TPU v7x, 256 devices: a whole 4x4x8 slice. The times are simulated.
256 devices in a mesh: dp: 16 (over y_hi, x, core), seq: 16 (over y_lo, z).
Axes of the slice: x: 4, y: 4 (y_hi: 2, y_lo: 2; y = y_hi * 2 + y_lo), z: 8, core: 2. Of those that a mesh axis runs over, the one named last changes fastest.
Arguments:
- tokens: bfloat16 [16, 4096, 1280], P('dp', 'seq'), may hold values from -6 to 6
- tube_index: int32 [16, 4096], P('dp', 'seq'), may hold values from 0 to 16383
- counts: int32 [16, 16], P('dp', 'seq'), may hold values from 128 to 256
- qkv_weight: bfloat16 [1280, 3840], P('dp'), may hold values from -4 to 4
- proj_weight: bfloat16 [1280, 1280], P('dp'), may hold values from -0.15625 to 0.15625
- ctx_b: bfloat16 [16, 4096, 1280], P('dp', 'seq'), may hold values from -12 to 12
- cot_b: bfloat16 [16, 4096, 1280], P('dp', 'seq'), may hold values from -12 to 12
- b_counts: int32 [16, 16], P('dp', 'seq'), may hold values from 128 to 256
Outputs:
- out_a: bfloat16 [16, 4096, 1280], P('dp', 'seq')
- weight_grad: float32 [1280, 1280], P('dp')
Inputs may be any that keep to these rules, and one draw needn't show every extreme that they name: `counts`: slots of a device's block past its count hold padding. `b_counts`: slots of a device's block past its count hold padding.
All inputs are finite; a program needn't handle non-finite values.
Results may differ from a plain program's by a relative error of at most 0.017.
Values may be sent and summed in bfloat16 or wider, within the bound.
No kernel may reach another device: no remote copies, remote signals or barrier semaphores. Data moves between devices by JAX's collectives and lax.ppermute only.
A program may use at most 128 MiB of HBM per device.

v0:
```python
import math
import jax
import jax.numpy as jnp
from jax import lax
from jax.sharding import Mesh
from jax.sharding import PartitionSpec as P

HEADS = 16
SEQ = ("seq_0", "seq_1")
DP = ("dp_0", "dp_1", "dp_2")


def in_order(parts, dim):
    shape = list(parts.shape[1:])
    shape[dim] *= parts.shape[0]
    return jnp.moveaxis(parts, 0, dim).reshape(shape)


def stacked_from(x, axes, sequence):
    parts = x
    for k in sequence:
        parts = lax.all_gather(parts, axes[k])
    done = sequence[::-1]
    back = [done.index(k) for k in range(len(axes))]
    parts = parts.transpose(*back, *range(len(axes), parts.ndim))
    return parts.reshape(-1, *x.shape)


def gathered_by_axis(x, axes, sequence, dim):
    return in_order(stacked_from(x, axes, sequence), dim)


def over_pieces(x, axis):
    return lax.all_gather(x, axis).astype(jnp.float32).sum(0)


def embed(tube_ids, model_width):
    half_width = model_width // 2
    positions = jnp.arange(half_width, dtype=jnp.float32)
    frequency = jnp.exp(positions * (-2.0 * math.log(10000.0) / model_width))
    angles = tube_ids.astype(jnp.float32)[:, None] * frequency[None, :]
    return jnp.concatenate([jnp.sin(angles), jnp.cos(angles)], axis=1)


def layer_norm(values):
    centered = values - jnp.mean(values, axis=1, keepdims=True)
    spread = jnp.mean(centered * centered, axis=1, keepdims=True)
    return centered * lax.rsqrt(spread + 1e-06)


def attend(grouped, valid_keys, heads_here, head_width):
    seq_length = grouped.shape[0]
    query_rows = grouped[:, 0].reshape(seq_length, heads_here, head_width)
    key_rows = grouped[:, 1].reshape(seq_length, heads_here, head_width)
    value_rows = grouped[:, 2].reshape(seq_length, heads_here, head_width)
    block_rows = math.gcd(seq_length, 512)
    score_scale = 1.0 / math.sqrt(head_width)
    blocked = query_rows.reshape(seq_length // block_rows, block_rows, heads_here, head_width)

    def one_block(block_query):
        scores = (
            jnp.einsum("qhd,khd->hqk", block_query, key_rows, preferred_element_type=jnp.float32)
            * score_scale
        )
        scores = jnp.where(valid_keys[None, None, :], scores, -1e30)
        top_score = jnp.max(scores, axis=2, keepdims=True)
        exponent = jnp.exp(scores - top_score)
        weights = (exponent / jnp.sum(exponent, axis=2, keepdims=True)).astype(jnp.bfloat16)
        return jnp.einsum(
            "hqk,khd->qhd", weights, value_rows, preferred_element_type=jnp.float32
        ).astype(jnp.bfloat16)

    return lax.map(one_block, blocked).reshape(seq_length, heads_here * head_width)


def on_device(tokens, tube_index, counts, qkv_weight, proj_weight, ctx_b, cot_b, b_counts):
    slot_cap = tokens.shape[1]
    model_width = tokens.shape[2]
    seq_count = lax.axis_size(SEQ)
    dp_count = lax.axis_size(DP)
    heads_here = HEADS // seq_count
    head_width = model_width // HEADS
    with_pos = tokens[0].astype(jnp.float32) + embed(tube_index[0], model_width)
    normed = layer_norm(with_pos).astype(jnp.bfloat16)
    columns = normed
    projected = jnp.dot(
        columns,
        lax.all_gather(qkv_weight, DP, axis=0, tiled=True),
        preferred_element_type=jnp.float32,
    ).astype(jnp.bfloat16)
    all_counts = gathered_by_axis(counts, SEQ, (0, 1), 1)
    slot_ids = lax.broadcasted_iota(jnp.int32, (1, slot_cap), 1)
    valid_keys = (slot_ids < all_counts[0][:, None]).reshape(seq_count * slot_cap)
    grouped = lax.all_to_all(
        projected.reshape(slot_cap, 3, model_width), SEQ, split_axis=2, concat_axis=0, tiled=True
    )
    head_context = attend(grouped, valid_keys, heads_here, head_width)
    context = lax.all_to_all(head_context, SEQ, split_axis=0, concat_axis=1, tiled=True)
    columns = context
    mixed = jnp.dot(
        columns, gathered_by_axis(proj_weight, DP, (0, 1, 2), 0), preferred_element_type=jnp.float32
    )
    out_a = (with_pos + mixed).astype(jnp.bfloat16)[None]
    row_ids = lax.broadcasted_iota(jnp.int32, (slot_cap, 1), 0)
    keep_rows = row_ids < b_counts[0, 0]
    masked_cot = jnp.where(keep_rows, cot_b[0], jnp.zeros((), jnp.bfloat16))
    factor = 1.0 / math.sqrt(dp_count * seq_count * slot_cap)
    column_part = ctx_b[0]
    own_rows = lax.psum_scatter(
        lax.dot_general(
            column_part, masked_cot, (((0,), (0,)), ((), ())), preferred_element_type=jnp.float32
        )
        * factor,
        DP,
        scatter_dimension=0,
        tiled=True,
    )
    weight_grad = over_pieces(own_rows.astype(jnp.bfloat16), SEQ).astype(jnp.float32)
    return (out_a, weight_grad)


def solution(mesh):
    split = Mesh(mesh.devices.reshape(2, 4, 2, 2, 8), ("dp_0", "dp_1", "dp_2", "seq_0", "seq_1"))
    return jax.shard_map(
        on_device,
        mesh=split,
        in_specs=(
            P(DP, SEQ, None),
            P(DP, SEQ),
            P(DP, SEQ),
            P(DP, None),
            P(DP, None),
            P(DP, SEQ, None),
            P(DP, SEQ, None),
            P(DP, SEQ),
        ),
        out_specs=(P(DP, SEQ, None), P(DP, None)),
        check_vma=False,
    )
```

profile of v0, /device:TPU:4, one launch (start us, length us, event | category | flops | bytes accessed | tf_op | source)
XLA Modules:
  0.0 355.5 jit_solution(13332053079246862315)
XLA Ops:
  8.0 10.9 %all-gather.2 = bf16[160,1280]{1,0:T(8,128)(2,1)} all-gather(bf16[80,1280]{1,0:T(8,128)(2,1)} %param.14), channel_id=4, replica_groups=mesh['dp_0'=2,'dp_1'=4,'dp_2'=2,'seq_0'=2,'seq_1'=8] {'dp_0'}, dimensions={0}, use_global_device_ids=true | all-gather | bytes 614400 | tf_op jit(solution)/shard_map/all_gather | solution.py:22
  19.6 5.0 %fusion.16 = f32[1280,1280]{0,1:T(8,128)} fusion(bf16[1,256,1280]{2,1,0:T(8,128)(2,1)S(1)} %copy-done, bf16[1,256,1280]{2,1,0:T(8,128)(2,1)} %param.16, pred[256]{0:T(512)(128)(4,1)S(1)} %iota_compare_fusion.1), kind=kOutput, calls=%fused_computation.20 | convolution fusion | flops 840826880 | bytes 7864576 | tf_op jit(solution)/shard_map/dot_general | solution.py:110
  24.6 8.3 %copy.45 = f32[1280,1280]{1,0:T(8,128)} copy(f32[1280,1280]{0,1:T(8,128)} %fusion.16) | data formatting | bytes 13107200
  33.5 2.3 multiply_sine_fusion
  36.5 59.3 %all-gather.11.cloned.1.call-done = bf16[1280,3840]{1,0:T(8,128)(2,1)} async-done(((bf16[80,3840]{1,0:T(8,128)(2,1)}), bf16[1280,3840]{1,0:T(8,128)(2,1)}) %all-gather.11.cloned.1.call-update) | async-done | bytes 9830416 | tf_op jit(solution)/shard_map/all_gather | solution.py:88
  95.8 7.9 %convolution_convert_fusion = bf16[256,3840]{1,0:T(8,128)(2,1)} fusion(bf16[1280,3840]{1,0:T(8,128)(2,1)} %all-gather.11.cloned.1.call-done, f32[256]{0:T(256)S(1)} %add_rsqrt_fusion, f32[256]{0:T(256)S(1)} %broadcast_multiply_fusion, f32[256,640]{1,0:T(8,128)S(1)} %get-tuple-element.86, f32[256,640]{1,0:T(8,128)S(1)} %get-tuple-element.85, ...), kind=kOutput, calls=%fused_computation.22 | convolution fusion | flops 2519531520 | bytes 13764608 | tf_op jit(solution)/shard_map/dot_general | solution.py:86
  103.6 2.7 copy.35
  106.3 11.2 %copy.36 = bf16[256,3,1280]{0,1,2:T(4,128)(2,1)} copy(bf16[256,3,1280]{0,2,1:T(8,128)(2,1)S(1)} %bitcast.93) | data formatting | bytes 3932160 | tf_op jit(solution)/shard_map/reshape | solution.py:95
  117.6 7.3 %all-to-all-start = ((bf16[256,3,1280]{0,1,2:T(4,128)(2,1)}), bf16[256,3,1280]{0,1,2:T(4,128)(2,1)S(1)}, u32[]{:S(2)}, u32[]{:S(2)}) async-start(bf16[256,3,1280]{0,1,2:T(4,128)(2,1)} %copy.36), calls=%async_computation | async-start | bytes 5242880 | tf_op jit(solution)/shard_map/all_to_all | solution.py:94
  127.6 4.5 %all-reduce = s32[2]{0:T(128)S(1)} all-reduce(s32[2]{0:T(128)S(1)} %bitcast_dynamic-update-slice_fusion), channel_id=2, replica_groups=mesh['dp_0'=2,'dp_1'=4,'dp_2'=2,'seq_0'=2,'seq_1'=8] {'seq_0'}, use_global_device_ids=true, to_apply=%add | all-reduce | flops 2 | bytes 16
  133.6 61.1 %all-reduce.1 = s32[16]{0:T(128)S(1)} all-reduce(s32[16]{0:T(128)S(1)} %dynamic-update-slice.1), channel_id=3, replica_groups=mesh['dp_0'=2,'dp_1'=4,'dp_2'=2,'seq_0'=2,'seq_1'=8] {'seq_1'}, use_global_device_ids=true, to_apply=%add.1 | all-reduce | flops 16 | bytes 128
  194.9 40.4 %reduce-scatter.4.cloned.1.call-done = f32[80,1280]{1,0:T(8,128)} async-done(((f32[1280,1280]{1,0:T(8,128)}), f32[80,1280]{1,0:T(8,128)}) %reduce-scatter.4.cloned.1.call-update) | async-done | bytes 409616 | tf_op jit(solution)/shard_map/reduce_scatter | solution.py:109
  238.7 50.4 %while.11 = (s32[]{:T(128)}, bf16[8,512,1,80]{1,3,2,0:T(8,128)(2,1)S(1)}, bf16[8,512,1,80]{1,3,2,0:T(8,128)(2,1)S(1)}, bf16[4096,1,80]{0,2,1:T(8,128)(2,1)S(1)},...) while((s32[]{:T(128)}, bf16[8,512,1,80]{1,3,2,0:T(8,128)(2,1)S(1)}, ...), condition=%wide.region_5.6_spmd.clone, body=%wide.region_2.5_spmd.clone.sunk | while | flops 696298496 | bytes 26675348 | solution.py:73
  240.3 2.2 fusion.38
  242.5 2.5 fusion.39
  246.6 2.2 fusion.38
  248.8 2.5 fusion.39
  252.9 2.2 fusion.38
  255.1 2.5 fusion.39
  259.2 2.2 fusion.38
  261.4 2.5 fusion.39
  265.5 2.2 fusion.38
  267.7 2.5 fusion.39
  271.8 2.2 fusion.38
  274.0 2.5 fusion.39
  280.3 2.5 fusion.39
  286.6 2.5 fusion.39
  290.7 7.2 %all-to-all-start.1 = ((bf16[16,256,80]{1,2,0:T(8,128)(2,1)}), bf16[16,256,80]{1,2,0:T(8,128)(2,1)S(1)}, u32[]{:S(2)}, u32[]{:S(2)}) async-start(bf16[16,256,80]{1,2,0:T(8,128)(2,1)} %copy.42), calls=%async_computation.1 | async-start | bytes 1310720 | tf_op jit(solution)/shard_map/all_to_all | solution.py:98
  297.9 4.0 %copy.43 = bf16[2,4,2,80,1280]{4,3,2,1,0:T(8,128)(2,1)} copy(bf16[2,4,2,80,1280]{4,3,0,1,2:T(8,128)(2,1)} %bitcast.95) | data formatting | bytes 6553600 | tf_op jit(solution)/shard_map/transpose | solution.py:25
  301.9 40.0 %all-gather.17.cloned.1.call-done = bf16[1280,1280]{1,0:T(8,128)(2,1)} async-done(((bf16[80,1280]{1,0:T(8,128)(2,1)}), bf16[1280,1280]{1,0:T(8,128)(2,1)}) %all-gather.17.cloned.1.call-update) | async-done | bytes 3276816 | tf_op jit(solution)/shard_map/all_gather | solution.py:34
  341.9 3.2 convert_reduce_fusion
  345.1 3.9 %fusion.18 = bf16[1,256,1280]{2,1,0:T(8,128)(2,1)} fusion(bf16[256,1280]{0,1:T(8,128)(2,1)S(1)} %bitcast.102, bf16[1280,1280]{1,0:T(8,128)(2,1)} %bitcast.97, f32[256,640]{1,0:T(8,128)S(1)} %copy-done.5, f32[256,640]{1,0:T(8,128)S(1)} %copy-done.3, bf16[1,256,1280]{2,1,0:T(8,128)(2,1)S(1)} %copy-done.7), kind=kOutput, calls=%fused_computation.25 | convolution fusion | flops 840499200 | bytes 6553600 | tf_op jit(solution)/shard_map/dot_general | solution.py:100
  (89 shorter events, 27.5 us)
Async XLA Ops:
  7.2 12.4 %copy-start = (bf16[1,256,1280]{2,1,0:T(8,128)(2,1)S(1)}, bf16[1,256,1280]{2,1,0:T(8,128)(2,1)}, u32[]{:S(2)}) copy-start(bf16[1,256,1280]{2,1,0:T(8,128)(2,1)} %param.15) | copy-start | bytes 1966084
  7.2 88.6 %all-gather.11.cloned.1.call-start = ((), (), s32[]{:S(2)}) async-start(), calls=%async_computation.3 | async-start | bytes 10444800 | tf_op jit(solution)/shard_map/all_gather | solution.py:88
  7.9 117.3 %all-gather.13.cloned.1.call-start = ((), (), s32[]{:S(2)}) async-start(), calls=%async_computation.4 | async-start | bytes 2048000 | tf_op jit(solution)/shard_map/all_gather | solution.py:22
  18.9 216.5 %reduce-scatter.4.cloned.1.call-start = ((), (), s32[]{:S(2)}) async-start(), calls=%async_computation.7 | async-start | bytes 6963200 | tf_op jit(solution)/shard_map/reduce_scatter | solution.py:109
  32.9 0.7 copy-start.9
  32.9 3.1 copy-start.6
  35.9 59.9 %copy-start.4 = (f32[256,640]{1,0:T(8,128)}, f32[256,640]{1,0:T(8,128)S(1)}, u32[]{:S(2)}) copy-start(f32[256,640]{1,0:T(8,128)S(1)} %get-tuple-element.86) | copy-start | bytes 1966084
  35.9 67.7 %copy-start.2 = (f32[256,640]{1,0:T(8,128)}, f32[256,640]{1,0:T(8,128)S(1)}, u32[]{:S(2)}) copy-start(f32[256,640]{1,0:T(8,128)S(1)} %get-tuple-element.85) | copy-start | bytes 1966084
  117.6 8.6 %copy-start.11 = (u32[256]{0:T(256)S(1)}, u32[256]{0:T(256)}, u32[]{:S(2)}) copy-start(u32[256]{0:T(256)} %constant.42) | copy-start | bytes 3076
  117.6 14.5 %copy-start.10 = (u32[256]{0:T(256)S(1)}, u32[256]{0:T(256)}, u32[]{:S(2)}) copy-start(u32[256]{0:T(256)} %constant.47) | copy-start | bytes 3076
  117.6 119.5 %all-to-all-start = ((bf16[256,3,1280]{0,1,2:T(4,128)(2,1)}), bf16[256,3,1280]{0,1,2:T(4,128)(2,1)S(1)}, u32[]{:S(2)}, u32[]{:S(2)}) async-start(bf16[256,3,1280]{0,1,2:T(4,128)(2,1)} %copy.36), calls=%async_computation | async-start | bytes 5242880 | tf_op jit(solution)/shard_map/all_to_all | solution.py:94
  124.8 173.1 %all-gather.15.cloned.1.call-start = ((), (), s32[]{:S(2)}) async-start(), calls=%async_computation.5 | async-start | bytes 4915200 | tf_op jit(solution)/shard_map/all_gather | solution.py:22
  125.4 216.5 %all-gather.17.cloned.1.call-start = ((), (), s32[]{:S(2)}) async-start(), calls=%async_computation.6 | async-start | bytes 3481600 | tf_op jit(solution)/shard_map/all_gather | solution.py:34
  237.6 1.1 copy-start.8
  290.7 54.4 %all-to-all-start.1 = ((bf16[16,256,80]{1,2,0:T(8,128)(2,1)}), bf16[16,256,80]{1,2,0:T(8,128)(2,1)S(1)}, u32[]{:S(2)}, u32[]{:S(2)}) async-start(bf16[16,256,80]{1,2,0:T(8,128)(2,1)} %copy.42), calls=%async_computation.1 | async-start | bytes 1310720 | tf_op jit(solution)/shard_map/all_to_all | solution.py:98
  301.9 43.2 %copy-start.3 = (f32[256,640]{1,0:T(8,128)S(1)}, f32[256,640]{1,0:T(8,128)}, u32[]{:S(2)}) copy-start(f32[256,640]{1,0:T(8,128)} %copy-done.2) | copy-start | bytes 1966084
  301.9 43.2 %copy-start.5 = (f32[256,640]{1,0:T(8,128)S(1)}, f32[256,640]{1,0:T(8,128)}, u32[]{:S(2)}) copy-start(f32[256,640]{1,0:T(8,128)} %copy-done.4) | copy-start | bytes 1966084
  301.9 43.2 %copy-start.7 = (bf16[1,256,1280]{2,1,0:T(8,128)(2,1)S(1)}, bf16[1,256,1280]{2,1,0:T(8,128)(2,1)}, u32[]{:S(2)}) copy-start(bf16[1,256,1280]{2,1,0:T(8,128)(2,1)} %param.10) | copy-start | bytes 1966084
  345.1 3.9 %copy-start.1 = (bf16[1,256,1280]{2,1,0:T(8,128)(2,1)S(1)}, bf16[1,256,1280]{2,1,0:T(8,128)(2,1)}, u32[]{:S(2)}) copy-start(bf16[1,256,1280]{2,1,0:T(8,128)(2,1)} %param.15) | copy-start | bytes 1966084
Sparse Core Ops, SparseCore 0:
  10.7 85.0 all-gather.10
  97.6 27.6 all-gather.12
  129.7 105.5 reduce-scatter.3
  237.0 18.0 all-gather.14
  257.3 84.5 all-gather.16
where the time goes:
time: 356 us
  waiting for transfers between devices  141 us (40%)
  blocking collectives  76.5 us (21%)
  matrix products  48.9 us (14%)
  local copies, waits for them, and re-layouts  32.7 us (9%)
  other arithmetic  25.7 us (7%)
  between operations  15.9 us (4%)
  starting transfers between devices  14.6 us (4%)
    unnamed x2, blocking collectives  65.6 us
    all_gather x1, waiting for transfers between devices, on_device(): lax.all_gather(qkv_weight, DP, axis=0, tiled=True)  59.3 us
    reduce_scatter x1, waiting for transfers between devices, on_device(): lax.psum_scatter(lax.dot_general(column_part, masked_cot, (((0,), (0,)),...  40.4 us
    all_gather x1, waiting for transfers between devices, over_pieces(): return lax.all_gather(x, axis).astype(jnp.float32).sum(0)  40 us
    dot_general x8, matrix products, one_block(): jnp.einsum('hqk,khd->qhd', weights, value_rows, preferred_element_type=jn...  19.9 us
    reduce_sum x8, other arithmetic, one_block(): jnp.sum(exponent, axis=2, keepdims=True)  17.3 us
    dot_general x8, matrix products, one_block(): jnp.einsum('qhd,khd->hqk', block_query, key_rows, preferred_element_type=...  12.3 us
    unnamed x31, local copies, waits for them, and re-layouts  12.1 us
  transfers between devices with their start and end apart: 7, of which 4 were waited for; matrix products, arithmetic and copies ran while one was open for 29% of the time, Pallas kernels for 0%

commit v1 on v0

--- a/solution.py
+++ b/solution.py
@@ -85,7 +85,9 @@
     columns = normed
     projected = jnp.dot(
         columns,
-        lax.all_gather(qkv_weight, DP, axis=0, tiled=True),
+        jnp.concatenate(
+            lax.all_to_all(jnp.stack([qkv_weight] * lax.axis_size(DP)), DP, 0, 0), axis=0
+        ),
         preferred_element_type=jnp.float32,
     ).astype(jnp.bfloat16)
     all_counts = gathered_by_axis(counts, SEQ, (0, 1), 1)

time: 356 us -> 374 us (1.051)
  local copies, waits for them, and re-layouts: 32.7 us -> 38.7 us
  starting transfers between devices: 14.6 us -> 19.1 us
    all_to_all x0 -> x1, waiting for transfers between devices: none -> 122 us  [on_device(): lax.all_to_all(jnp.stack([qkv_weight] * lax.axis_size(DP)), DP, 0, 0)]
    all_gather x1 -> x0, waiting for transfers between devices: 59.3 us -> none  [on_device(): lax.all_gather(qkv_weight, DP, axis=0, tiled=True)]
    reduce_scatter x1, waiting for transfers between devices: 40.4 us -> 0.01 us  [on_device(): lax.psum_scatter(lax.dot_general(column_part, masked_cot, (((0,), (0,)),...]
    all_gather x1, waiting for transfers between devices: 40 us -> 1.87 us  [over_pieces(): return lax.all_gather(x, axis).astype(jnp.float32).sum(0)]
    all_to_all x1, waiting for transfers between devices: 0.01 us -> 17.8 us  [on_device(): lax.all_to_all(head_context, SEQ, split_axis=0, concat_axis=1, tiled=True)]
    all_to_all x0 -> x1, starting transfers between devices: none -> 6.03 us  [on_device(): lax.all_to_all(jnp.stack([qkv_weight] * lax.axis_size(DP)), DP, 0, 0)]
    another operation x0 -> x1, local copies, waits for them, and re-layouts: none -> 5.47 us  [on_device(): jnp.stack([qkv_weight] * lax.axis_size(DP))]
    unnamed x31 -> x33, local copies, waits for them, and re-layouts: 12.1 us -> 12.5 us
  transfers between devices with their start and end apart: 7 -> 7, of which waited for: 4 -> 3; matrix products, arithmetic and copies ran while one was open for 29% -> 29% of each run, Pallas kernels for 0% -> 0%
where the time goes in v1:
time: 374 us; the launch traced here: 371 us
  waiting for transfers between devices  143 us (38%)
  blocking collectives  76.6 us (20%)
  matrix products  47.9 us (13%)
  local copies, waits for them, and re-layouts  38.7 us (10%)
  other arithmetic  28.1 us (8%)
  starting transfers between devices  19.1 us (5%)
  between operations  17.4 us (5%)
    all_to_all x1, waiting for transfers between devices, on_device(): lax.all_to_all(jnp.stack([qkv_weight] * lax.axis_size(DP)), DP, 0, 0)  122 us
    unnamed x2, blocking collectives  65.6 us
    dot_general x8, matrix products, one_block(): jnp.einsum('hqk,khd->qhd', weights, value_rows, preferred_element_type=jn...  19.9 us
    all_to_all x1, waiting for transfers between devices, on_device(): lax.all_to_all(head_context, SEQ, split_axis=0, concat_axis=1, tiled=True)  17.8 us
    reduce_sum x8, other arithmetic, one_block(): jnp.sum(exponent, axis=2, keepdims=True)  17.3 us
    unnamed x33, local copies, waits for them, and re-layouts  12.5 us
    dot_general x8, matrix products, one_block(): jnp.einsum('qhd,khd->hqk', block_query, key_rows, preferred_element_type=...  12.3 us
    reshape x1, local copies, waits for them, and re-layouts, on_device(): projected.reshape(slot_cap, 3, model_width)  11.4 us
  transfers between devices with their start and end apart: 7, of which 3 were waited for; matrix products, arithmetic and copies ran while one was open for 29% of the time, Pallas kernels for 0%

profile of v1, /device:TPU:4, one launch (start us, length us, event | category | flops | bytes accessed | tf_op | source)
XLA Modules:
  0.0 370.8 jit_solution(2713881374877188662)
XLA Ops:
  8.1 11.0 %all-gather.2 = bf16[160,1280]{1,0:T(8,128)(2,1)} all-gather(bf16[80,1280]{1,0:T(8,128)(2,1)} %param.14), channel_id=4, replica_groups=mesh['dp_0'=2,'dp_1'=4,'dp_2'=2,'seq_0'=2,'seq_1'=8] {'dp_0'}, dimensions={0}, use_global_device_ids=true | all-gather | bytes 614400 | tf_op jit(solution)/shard_map/all_gather | solution.py:22
  19.1 5.5 %stack.2 = bf16[16,80,3840]{2,1,0:T(8,128)(2,1)} broadcast(bf16[80,3840]{1,0:T(8,128)(2,1)} %param.13), dimensions={1,2} | broadcast | bytes 10444800 | tf_op jit(solution)/shard_map/stack | solution.py:89
  24.5 6.0 %all-to-all-start = ((bf16[16,80,3840]{2,1,0:T(8,128)(2,1)}), bf16[16,80,3840]{2,1,0:T(8,128)(2,1)}, u32[]{:S(2)}, u32[]{:S(2)}) async-start(bf16[16,80,3840]{2,1,0:T(8,128)(2,1)} %stack.2), calls=%async_computation | async-start | bytes 19660800 | tf_op jit(solution)/shard_map/all_to_all | solution.py:89
  31.3 3.9 %fusion.16 = f32[1280,1280]{0,1:T(8,128)} fusion(bf16[1,256,1280]{2,1,0:T(8,128)(2,1)S(1)} %copy-done, bf16[1,256,1280]{2,1,0:T(8,128)(2,1)S(1)} %copy-done.8, pred[256]{0:T(512)(128)(4,1)S(1)} %iota_compare_fusion.1), kind=kOutput, calls=%fused_computation.20 | convolution fusion | flops 840826880 | bytes 7864576 | tf_op jit(solution)/shard_map/dot_general | solution.py:112
  35.2 8.2 %copy.45 = f32[1280,1280]{1,0:T(8,128)} copy(f32[1280,1280]{0,1:T(8,128)} %fusion.16) | data formatting | bytes 13107200
  44.1 2.3 multiply_sine_fusion.1
  47.6 2.3 multiply_sine_fusion
  50.0 122.3 %all-to-all-done = bf16[16,80,3840]{2,1,0:T(8,128)(2,1)} async-done(((bf16[16,80,3840]{2,1,0:T(8,128)(2,1)}), bf16[16,80,3840]{2,1,0:T(8,128)(2,1)}, u32[]{:S(2)}, u32[]{:S(2)}) %all-to-all-start) | async-done | bytes 9830432 | tf_op jit(solution)/shard_map/all_to_all | solution.py:89
  172.4 7.9 %convolution_convert_fusion = bf16[256,3840]{1,0:T(8,128)(2,1)} fusion(bf16[1280,3840]{1,0:T(8,128)(2,1)} %bitcast.3, f32[1,256,640]{2,1,0:T(8,128)S(1)} %get-tuple-element.88, f32[1,256,640]{2,1,0:T(8,128)S(1)} %get-tuple-element.87, bf16[1,256,1280]{2,1,0:T(8,128)(2,1)S(1)} %copy-done.6, f32[256]{0:T(256)S(1)} %add_rsqrt_fusion, ...), kind=kOutput, calls=%fused_computation.22 | convolution fusion | flops 2519531520 | bytes 13764608 | tf_op jit(solution)/shard_map/dot_general | solution.py:86
  180.2 2.7 copy.35
  182.9 11.4 %copy.36 = bf16[256,3,1280]{0,1,2:T(4,128)(2,1)} copy(bf16[256,3,1280]{0,2,1:T(8,128)(2,1)S(1)} %bitcast.95) | data formatting | bytes 3932160 | tf_op jit(solution)/shard_map/reshape | solution.py:97
  194.3 9.2 %all-to-all-start.1 = ((bf16[256,3,1280]{0,1,2:T(4,128)(2,1)}), bf16[256,3,1280]{0,1,2:T(4,128)(2,1)S(1)}, u32[]{:S(2)}, u32[]{:S(2)}) async-start(bf16[256,3,1280]{0,1,2:T(4,128)(2,1)} %copy.36), calls=%async_computation.1 | async-start | bytes 5242880 | tf_op jit(solution)/shard_map/all_to_all | solution.py:96
  206.2 4.6 %all-reduce = s32[2]{0:T(128)S(1)} all-reduce(s32[2]{0:T(128)S(1)} %bitcast_dynamic-update-slice_fusion), channel_id=2, replica_groups=mesh['dp_0'=2,'dp_1'=4,'dp_2'=2,'seq_0'=2,'seq_1'=8] {'seq_0'}, use_global_device_ids=true, to_apply=%add | all-reduce | flops 2 | bytes 16
  212.3 61.1 %all-reduce.1 = s32[16]{0:T(128)S(1)} all-reduce(s32[16]{0:T(128)S(1)} %dynamic-update-slice.1), channel_id=3, replica_groups=mesh['dp_0'=2,'dp_1'=4,'dp_2'=2,'seq_0'=2,'seq_1'=8] {'seq_1'}, use_global_device_ids=true, to_apply=%add.1 | all-reduce | flops 16 | bytes 128
  277.0 50.4 %while.11 = (s32[]{:T(128)}, bf16[8,512,1,80]{1,3,2,0:T(8,128)(2,1)S(1)}, bf16[8,512,1,80]{1,3,2,0:T(8,128)(2,1)S(1)}, bf16[4096,1,80]{0,2,1:T(8,128)(2,1)S(1)},...) while((s32[]{:T(128)}, bf16[8,512,1,80]{1,3,2,0:T(8,128)(2,1)S(1)}, ...), condition=%wide.region_5.6_spmd.clone, body=%wide.region_2.5_spmd.clone.sunk | while | flops 696298496 | bytes 26675356 | solution.py:73
  278.6 2.2 fusion.45
  280.8 2.5 fusion.46
  284.9 2.2 fusion.45
  287.1 2.5 fusion.46
  291.2 2.2 fusion.45
  293.4 2.5 fusion.46
  299.7 2.5 fusion.46
  306.0 2.5 fusion.46
  312.3 2.5 fusion.46
  318.6 2.5 fusion.46
  322.7 2.2 fusion.45
  324.9 2.5 fusion.46
  329.0 3.8 %all-to-all-start.2 = ((bf16[16,256,80]{1,2,0:T(8,128)(2,1)}), bf16[16,256,80]{1,2,0:T(8,128)(2,1)S(1)}, u32[]{:S(2)}, u32[]{:S(2)}) async-start(bf16[16,256,80]{1,2,0:T(8,128)(2,1)} %copy.42), calls=%async_computation.2 | async-start | bytes 1310720 | tf_op jit(solution)/shard_map/all_to_all | solution.py:100
  332.9 4.1 %copy.43 = bf16[2,4,2,80,1280]{4,3,2,1,0:T(8,128)(2,1)} copy(bf16[2,4,2,80,1280]{4,3,0,1,2:T(8,128)(2,1)} %bitcast.97) | data formatting | bytes 6553600 | tf_op jit(solution)/shard_map/transpose | solution.py:25
  336.9 17.8 %all-to-all-done.2 = bf16[16,256,80]{1,2,0:T(8,128)(2,1)S(1)} async-done(((bf16[16,256,80]{1,2,0:T(8,128)(2,1)}), bf16[16,256,80]{1,2,0:T(8,128)(2,1)S(1)}, u32[]{:S(2)}, u32[]{:S(2)}) %all-to-all-start.2) | async-done | bytes 655392 | tf_op jit(solution)/shard_map/all_to_all | solution.py:100
  354.7 3.9 %fusion.18 = bf16[1,256,1280]{2,1,0:T(8,128)(2,1)} fusion(bf16[256,1280]{0,1:T(8,128)(2,1)S(1)} %bitcast.104, bf16[1280,1280]{1,0:T(8,128)(2,1)} %bitcast.99, f32[256,640]{1,0:T(8,128)S(1)} %copy-done.5, f32[256,640]{1,0:T(8,128)S(1)} %copy-done.3, bf16[1,256,1280]{2,1,0:T(8,128)(2,1)S(1)} %copy-done.7), kind=kOutput, calls=%fused_computation.25 | convolution fusion | flops 840499200 | bytes 6553600 | tf_op jit(solution)/shard_map/dot_general | solution.py:102
  360.5 3.2 convert_reduce_fusion
  (92 shorter events, 33.5 us)
Async XLA Ops:
  8.0 23.3 %copy-start = (bf16[1,256,1280]{2,1,0:T(8,128)(2,1)S(1)}, bf16[1,256,1280]{2,1,0:T(8,128)(2,1)}, u32[]{:S(2)}) copy-start(bf16[1,256,1280]{2,1,0:T(8,128)(2,1)} %param.15) | copy-start | bytes 1966084
  8.0 195.6 %all-gather.10.cloned.1.call-start = ((), (), s32[]{:S(2)}) async-start(), calls=%async_computation.4 | async-start | bytes 2048000 | tf_op jit(solution)/shard_map/all_gather | solution.py:22
  24.5 6.7 %copy-start.8 = (bf16[1,256,1280]{2,1,0:T(8,128)(2,1)S(1)}, bf16[1,256,1280]{2,1,0:T(8,128)(2,1)}, u32[]{:S(2)}) copy-start(bf16[1,256,1280]{2,1,0:T(8,128)(2,1)} %param.16) | copy-start | bytes 1966084
  24.5 147.8 %all-to-all-start = ((bf16[16,80,3840]{2,1,0:T(8,128)(2,1)}), bf16[16,80,3840]{2,1,0:T(8,128)(2,1)}, u32[]{:S(2)}, u32[]{:S(2)}) async-start(bf16[16,80,3840]{2,1,0:T(8,128)(2,1)} %stack.2), calls=%async_computation | async-start | bytes 19660800 | tf_op jit(solution)/shard_map/all_to_all | solution.py:89
  30.6 243.0 %reduce-scatter.4.cloned.1.call-start = ((), (), s32[]{:S(2)}) async-start(), calls=%async_computation.7 | async-start | bytes 6963200 | tf_op jit(solution)/shard_map/reduce_scatter | solution.py:111
  43.4 0.7 copy-start.10
  43.4 3.1 copy-start.6
  46.5 0.8 copy-start.4
  46.5 133.7 %copy-start.2 = (f32[256,640]{1,0:T(8,128)}, f32[256,640]{1,0:T(8,128)S(1)}, u32[]{:S(2)}) copy-start(f32[256,640]{1,0:T(8,128)S(1)} %get-tuple-element.85) | copy-start | bytes 1966084
  194.3 10.6 %copy-start.12 = (u32[256]{0:T(256)S(1)}, u32[256]{0:T(256)}, u32[]{:S(2)}) copy-start(u32[256]{0:T(256)} %constant.42) | copy-start | bytes 3076
  194.3 16.5 %copy-start.11 = (u32[256]{0:T(256)S(1)}, u32[256]{0:T(256)}, u32[]{:S(2)}) copy-start(u32[256]{0:T(256)} %constant.47) | copy-start | bytes 3076
  194.3 81.0 %all-to-all-start.1 = ((bf16[256,3,1280]{0,1,2:T(4,128)(2,1)}), bf16[256,3,1280]{0,1,2:T(4,128)(2,1)S(1)}, u32[]{:S(2)}, u32[]{:S(2)}) async-start(bf16[256,3,1280]{0,1,2:T(4,128)(2,1)} %copy.36), calls=%async_computation.1 | async-start | bytes 5242880 | tf_op jit(solution)/shard_map/all_to_all | solution.py:96
  203.5 129.3 %all-gather.12.cloned.1.call-start = ((), (), s32[]{:S(2)}) async-start(), calls=%async_computation.5 | async-start | bytes 4915200 | tf_op jit(solution)/shard_map/all_gather | solution.py:22
  204.3 156.3 %all-gather.14.cloned.1.call-start = ((), (), s32[]{:S(2)}) async-start(), calls=%async_computation.6 | async-start | bytes 3481600 | tf_op jit(solution)/shard_map/all_gather | solution.py:34
  275.9 1.1 copy-start.9
  329.0 25.7 %all-to-all-start.2 = ((bf16[16,256,80]{1,2,0:T(8,128)(2,1)}), bf16[16,256,80]{1,2,0:T(8,128)(2,1)S(1)}, u32[]{:S(2)}, u32[]{:S(2)}) async-start(bf16[16,256,80]{1,2,0:T(8,128)(2,1)} %copy.42), calls=%async_computation.2 | async-start | bytes 1310720 | tf_op jit(solution)/shard_map/all_to_all | solution.py:100
  332.8 21.9 %copy-start.3 = (f32[256,640]{1,0:T(8,128)S(1)}, f32[256,640]{1,0:T(8,128)}, u32[]{:S(2)}) copy-start(f32[256,640]{1,0:T(8,128)} %copy-done.2) | copy-start | bytes 1966084
  332.8 21.9 %copy-start.5 = (f32[256,640]{1,0:T(8,128)S(1)}, f32[256,640]{1,0:T(8,128)}, u32[]{:S(2)}) copy-start(f32[256,640]{1,0:T(8,128)} %copy-done.4) | copy-start | bytes 1966084
  332.8 21.9 %copy-start.7 = (bf16[1,256,1280]{2,1,0:T(8,128)(2,1)S(1)}, bf16[1,256,1280]{2,1,0:T(8,128)(2,1)}, u32[]{:S(2)}) copy-start(bf16[1,256,1280]{2,1,0:T(8,128)(2,1)} %param.10) | copy-start | bytes 1966084
  354.7 9.0 %copy-start.1 = (bf16[1,256,1280]{2,1,0:T(8,128)(2,1)S(1)}, bf16[1,256,1280]{2,1,0:T(8,128)(2,1)}, u32[]{:S(2)}) copy-start(bf16[1,256,1280]{2,1,0:T(8,128)(2,1)} %param.15) | copy-start | bytes 1966084
Sparse Core Ops, SparseCore 0:
  19.2 52.8 all-gather.9
  206.1 23.5 all-gather.11
  275.5 85.0 all-gather.13
Sparse Core Ops, SparseCore 1:
  43.5 155.6 reduce-scatter.3
